TPU v7x, 8 devices: a whole 2x2x1 slice. The times are simulated.
8 devices in a mesh: dp: 1 (over z), sp: 8 (over x, y, core).
Axes of the slice: x: 2, y: 2, z: 1, core: 2. Of those that a mesh axis runs over, the one named last changes fastest.
Arguments:
- q: bfloat16 [32, 32, 160], P('dp')
- k: bfloat16 [32, 8192, 8, 160], P('dp', 'sp')
- v: bfloat16 [32, 8192, 8, 160], P('dp', 'sp')
Outputs:
- q: bfloat16 [32, 32, 160], P('dp')
All inputs are finite; a program needn't handle non-finite values.
Results may differ from a plain program's by a relative error of at most 0.012.
Values are sent between devices in bfloat16 or wider.
A program may use at most 2 GiB of HBM per device.

v0:
```python
import jax
import jax.numpy as jnp
from jax import lax
from jax.sharding import PartitionSpec as P


def einsum(form, a, b):
    return jnp.einsum(form, a.astype(jnp.float32), b.astype(jnp.float32))


def part_of(q, k, v):
    grouped = q.reshape(q.shape[0], k.shape[2], -1, q.shape[2])
    scores = einsum("bgsd,bugd->bgsu", grouped, k) * q.shape[2] ** -0.5
    high = jnp.max(scores, -1, keepdims=True)
    weights = jnp.exp(scores - high)
    seen = einsum("bgsu,bugd->bgsd", weights.astype(jnp.bfloat16), v)
    return jnp.concatenate([seen, jnp.sum(weights, -1, keepdims=True), high], -1)


def together(parts):
    seen, total, high = parts[..., :-2], parts[..., -2:-1], parts[..., -1:]
    scale = jnp.exp(high - jnp.max(high, 0))
    return (jnp.sum(seen * scale, 0) / jnp.sum(total * scale, 0)).astype(jnp.bfloat16)


def solution(mesh):
    def step(q, k, v):
        return together(lax.all_gather(part_of(q, k, v), "sp")).reshape(q.shape)

    return jax.shard_map(
        step,
        mesh=mesh,
        in_specs=(P("dp", None, None), P("dp", "sp", None, None), P("dp", "sp", None, None)),
        out_specs=P("dp", None, None),
        check_vma=False,
    )
```

profile of v0, /device:TPU:0, one launch (start us, length us, event | category | flops | bytes accessed | tf_op | source)
XLA Modules:
  0.0 159.7 jit_solution(9878577201117713541)
XLA Ops:
  6.5 0.0 all-gather.3.cloned.1.call-start
  6.5 1.2 reshape.15
  7.7 30.1 %multiply_reduce_fusion = (f32[32,8,4]{2,1,0:T(8,128)S(1)}, f32[32,8,4,1024]{3,2,1,0:T(4,128)}) fusion(bf16[32,8,4,160]{3,2,1,0:T(4,128)(2,1)S(1)} %reshape.15, bf16[32,1024,8,160]{1,3,2,0:T(8,128)(2,1)} %param.4), kind=kOutput, calls=%fused_computation.3 | convolution fusion | flops 337640448 | bytes 88412160 | tf_op jit(solution)/shard_map/bgsd,bugd->bgsu/dot_general | solution.py:8
  37.8 3.6 %fusion.1 = f32[32,8,4]{2,1,0:T(8,128)S(1)} fusion(f32[32,8,4,1024]{3,2,1,0:T(4,128)} %get-tuple-element.11, f32[32,8,4]{2,1,0:T(8,128)S(1)} %get-tuple-element.10), kind=kLoop, calls=%fused_computation.4 | loop fusion | flops 3144704 | bytes 4202496 | tf_op jit(solution)/shard_map/reduce_sum | solution.py:17
  41.4 32.0 %fusion.3 = f32[32,8,4,160]{3,2,1,0:T(4,128)S(1)} fusion(bf16[32,1024,8,160]{1,3,2,0:T(8,128)(2,1)} %param.5, f32[32,8,4,1024]{3,2,1,0:T(4,128)} %get-tuple-element.11, f32[32,8,4]{2,1,0:T(8,128)S(1)} %get-tuple-element.10), kind=kOutput, calls=%fused_computation.6 | convolution fusion | flops 338690048 | bytes 88739840 | tf_op jit(solution)/shard_map/bgsu,bugd->bgsd/dot_general | solution.py:8
  73.5 1.7 %copy.51 = f32[32,8,4,1]{3,2,1,0:T(4,128)S(1)} copy(f32[32,8,4,1]{2,1,0,3:T(8,128)S(1)} %bitcast.16) | data formatting | bytes 8192 | tf_op jit(solution)/shard_map/broadcast_in_dim | solution.py:17
  75.1 1.7 %copy.52 = f32[32,8,4,1]{3,2,1,0:T(4,128)S(1)} copy(f32[32,8,4,1]{2,1,0,3:T(8,128)S(1)} %bitcast.15) | data formatting | bytes 8192 | tf_op jit(solution)/shard_map/broadcast_in_dim | solution.py:14
  76.8 0.7 pad_maximum_fusion
  77.5 1.3 copy.53
  78.7 0.0 all-gather.3.cloned.1.call-update
  78.8 51.3 %all-gather.3.cloned.1.call-done = f32[256,8,4,162]{3,1,2,0:T(8,128)} async-done(((f32[32,8,4,162]{3,1,2,0:T(8,128)}), f32[256,8,4,162]{3,1,2,0:T(8,128)}) %all-gather.3.cloned.1.call-update) | async-done | bytes 5308432 | tf_op jit(solution)/shard_map/all_gather | solution.py:28
  130.1 8.9 %fusion.10 = (f32[8,32,8,4,1]{4,2,3,1,0:T(8,128)}, f32[32,8,4]{1,2,0:T(4,128)S(1)}, f32[8,32,8,4,1]{4,2,3,1,0:T(8,128)}) fusion(f32[8,32,8,4,162]{4,2,3,1,0:T(8,128)} %bitcast.13), kind=kLoop, calls=%fused_computation.17 | loop fusion | flops 7168 | bytes 135168 | tf_op jit(solution)/shard_map/slice | solution.py:21
  139.0 3.6 %copy.65 = f32[8,32,8,4,1]{1,2,4,3,0:T(8,128)S(1)} copy(f32[8,32,8,4,1]{4,2,3,1,0:T(8,128)} %get-tuple-element.5) | data formatting | bytes 65536
  142.6 0.1 copy.66
  142.7 3.7 %copy.64 = f32[8,32,8,4,1]{1,2,4,3,0:T(8,128)S(1)} copy(f32[8,32,8,4,1]{4,2,3,1,0:T(8,128)} %get-tuple-element.7) | data formatting | bytes 65536
  146.5 0.2 copy.55
  146.7 4.2 %fusion = f32[32,8,4,160]{3,1,2,0:T(8,128)S(1)} fusion(f32[8,32,8,4,162]{4,2,3,1,0:T(8,128)} %bitcast.14, f32[8,32,8,4]{2,3,1,0:T(4,128)S(1)} %copy.55), kind=kLoop, calls=%fused_computation.1 | loop fusion | flops 2457600 | bytes 5931008 | tf_op jit(solution)/shard_map/reduce_sum | solution.py:23
  150.9 0.6 copy.56
  151.5 0.2 fusion.7
  151.7 1.1 copy.59
  (2 shorter events, 0.0 us)
Async XLA Ops:
  6.5 123.5 %all-gather.3.cloned.1.call-start = ((), (), s32[]{:S(2)}) async-start(), calls=%async_computation | async-start | bytes 9437184 | tf_op jit(solution)/shard_map/all_gather | solution.py:28
Sparse Core Ops, SparseCore 0:
  78.9 51.1 all-gather.2
where the time goes:
time: 160 us
  matrix products  62.1 us (39%)
  waiting for transfers between devices  51.3 us (32%)
  other arithmetic  17.6 us (11%)
  local copies, waits for them, and re-layouts  15.2 us (10%)
  between operations  13.5 us (8%)
    dot_general x2, matrix products, einsum(): return jnp.einsum(form, a.astype(jnp.float32), b.astype(jnp.float32))  62.1 us
    all_gather x1, waiting for transfers between devices, step(): return together(lax.all_gather(part_of(q, k, v), 'sp')).reshape(q.shape)  51.3 us
    slice x1, other arithmetic, together(): seen, total, high = (parts[..., :-2], parts[..., -2:-1], parts[..., -1:])  8.92 us
    unnamed x3, local copies, waits for them, and re-layouts  7.41 us
    reduce_sum x1, other arithmetic, together(): jnp.sum(seen * scale, 0) / jnp.sum(total * scale, 0)  4.16 us
    reduce_sum x1, other arithmetic, part_of(): jnp.sum(weights, -1, keepdims=True)  3.62 us
  transfers between devices with their start and end apart: 1, of which 1 were waited for; matrix products, arithmetic and copies ran while one was open for 0% of the time, Pallas kernels for 0%

commit v1 on v0

v1 whole, which is shorter than its diff:
```python
import functools

import jax
import jax.numpy as jnp
from jax import lax
from jax.experimental import pallas as pl
from jax.experimental.pallas import tpu as pltpu
from jax.sharding import PartitionSpec as P

GROUP = 4
LANES = 128
MESH = pl.DeviceIdType.MESH


def kernel(n, axis, q_hbm, k_hbm, v_hbm, o_ref, q_buf, k_buf, v_buf, weights, highs, totals, parts, stats, q_sem, k_sem, v_sem,
           part_send, part_recv, stat_send, stat_recv):
    seqs, heads, head = q_buf.shape
    wide = k_buf.shape[1]
    kv_heads = wide // head
    share = heads // kv_heads
    rest = head - LANES
    groups = seqs // GROUP
    me = lax.axis_index(axis)

    barrier = pltpu.get_barrier_semaphore()
    for step in range(1, n):
        pl.semaphore_signal(barrier, inc=1, device_id={axis: lax.rem(me + step, n)}, device_id_type=MESH)

    def k_copy(seq, slot):
        return pltpu.make_async_copy(k_hbm.at[seq], k_buf.at[slot], k_sem.at[slot])

    def v_copy(seq, slot):
        return pltpu.make_async_copy(v_hbm.at[seq], v_buf.at[slot], v_sem.at[slot])

    q_copy = pltpu.make_async_copy(q_hbm, q_buf, q_sem)
    q_copy.start()
    for seq in range(GROUP):
        k_copy(seq, seq).start()
        v_copy(seq, seq).start()
    q_copy.wait()

    row = lax.broadcasted_iota(jnp.int32, (heads, wide), 0)
    lane = lax.broadcasted_iota(jnp.int32, (heads, wide), 1)
    first = (row // share) * head
    own = (lane >= first) & (lane < first + head)
    upper = lax.broadcasted_iota(jnp.int32, (2 * share, head), 0) < share
    place = lax.broadcasted_iota(jnp.int32, (heads, LANES), 1)

    def score(seq, slot):
        q = q_buf[seq].astype(jnp.float32)
        spread = jnp.where(own, jnp.concatenate([q] * kv_heads, axis=1), 0.0).astype(jnp.bfloat16)
        scores = jnp.dot(spread, k_buf[slot], preferred_element_type=jnp.float32) * head**-0.5
        high = jnp.max(scores, axis=1, keepdims=True)
        w = jnp.exp(scores - high)
        weights[slot] = w.astype(jnp.bfloat16)
        highs[slot] = jnp.broadcast_to(high, (heads, LANES))
        totals[slot] = jnp.broadcast_to(jnp.sum(w, axis=1, keepdims=True), (heads, LANES))

    def attend(slot):
        seen = lax.dot_general(weights[slot], v_buf[slot], (((1,), (1,)), ((), ())), preferred_element_type=jnp.float32)
        out = []
        for pair in range(kv_heads // 2):
            block = seen[2 * share * pair : 2 * share * (pair + 1), 2 * head * pair : 2 * head * (pair + 1)]
            out.append(jnp.where(upper, block[:, :head], block[:, head:]))
        return jnp.concatenate(out, axis=0)

    def share_out(group):
        for what, send, recv in ((parts, part_send, part_recv), (stats, stat_send, stat_recv)):
            for step in range(1, n):
                pltpu.make_async_remote_copy(
                    src_ref=what.at[group, me],
                    dst_ref=what.at[group, me],
                    send_sem=send,
                    recv_sem=recv.at[group, step - 1],
                    device_id={axis: lax.rem(me + step, n)},
                    device_id_type=MESH,
                ).start()

    def combine(group):
        for step in range(1, n):
            there = lax.rem(me + n - step, n)
            for what, recv in ((parts, part_recv), (stats, stat_recv)):
                ref = what.at[group, there]
                pltpu.make_async_copy(ref, ref, recv.at[group, step - 1]).wait()
        high = [stats[group, d, :GROUP, :] for d in range(n)]
        total = [stats[group, d, GROUP:, :] for d in range(n)]
        top = functools.reduce(jnp.maximum, high)
        scale = [jnp.exp(h - top) for h in high]
        inverse = 1.0 / functools.reduce(jnp.add, [t * s for t, s in zip(total, scale)])
        columns = jnp.transpose(jnp.concatenate([s * inverse for s in scale], axis=0))
        main = [jnp.zeros((heads, LANES), jnp.float32) for _ in range(GROUP)]
        tail = jnp.zeros((heads, LANES), jnp.float32)
        for d in range(n):
            mixed = None
            for j in range(GROUP):
                at = d * GROUP + j
                column = jnp.broadcast_to(columns[:heads, at : at + 1], (heads, LANES))
                main[j] += column * parts[group, d, heads * j : heads * (j + 1), :].astype(jnp.float32)
                mixed = column if mixed is None else jnp.where(place < rest * j, mixed, column)
            tail += mixed * parts[group, d, heads * GROUP :, :].astype(jnp.float32)
        for j in range(GROUP):
            o_ref[group * GROUP + j] = jnp.concatenate([main[j], tail[:, rest * j : rest * (j + 1)]], axis=1).astype(o_ref.dtype)

    def run(group, last):
        tails, table = [], jnp.zeros((heads, LANES), jnp.float32)
        for j in range(GROUP):
            seq, ahead = group * GROUP + j, (j + 1) % GROUP
            scores_next = not (last and j == GROUP - 1)
            if scores_next:
                k_copy(seq + 1, ahead).wait()
            v_copy(seq, j).wait()
            table = jnp.where(place == j, highs[j], table)
            table = jnp.where(place == GROUP + j, totals[j], table)
            if scores_next:
                score(seq + 1, ahead)
            out = attend(j)
            parts[group, me, heads * j : heads * (j + 1), :] = out[:, :LANES].astype(jnp.bfloat16)
            tails.append(out[:, LANES:])
            if not last:
                @pl.when(seq + 1 + GROUP < seqs)
                def _():
                    k_copy(seq + 1 + GROUP, ahead).start()

                v_copy(seq + GROUP, j).start()
        parts[group, me, heads * GROUP :, :] = jnp.concatenate(tails, axis=1).astype(jnp.bfloat16)
        turned = jnp.transpose(table)[: 2 * GROUP, :]
        stats[group, me] = jnp.concatenate([turned, jnp.zeros((2 * GROUP, LANES - heads), jnp.float32)], axis=1)

    k_copy(0, 0).wait()
    score(0, 0)
    k_copy(GROUP, 0).start()
    run(0, False)
    pl.semaphore_wait(barrier, n - 1)
    share_out(0)

    def middle(group, carry):
        run(group, False)
        share_out(group)
        combine(group - 1)
        return carry

    lax.fori_loop(1, groups - 1, middle, 0)
    run(groups - 1, True)
    share_out(groups - 1)
    combine(groups - 2)
    combine(groups - 1)
    for what, send in ((parts, part_send), (stats, stat_send)):
        ref = what.at[:, pl.ds(0, n - 1)]
        pltpu.make_async_copy(ref, ref, send).wait()


def attention(n, axis, q, k, v):
    seqs, run, kv_heads, head = k.shape
    heads = q.shape[1]
    groups = seqs // GROUP
    k, v = (x.transpose(0, 2, 3, 1).reshape(seqs, kv_heads * head, run) for x in (k, v))
    q, k, v = (pltpu.with_memory_space_constraint(x, pltpu.HBM) for x in (q, k, v))
    return pl.pallas_call(
        functools.partial(kernel, n, axis),
        out_shape=jax.ShapeDtypeStruct(q.shape, jnp.bfloat16),
        in_specs=[pl.BlockSpec(memory_space=pltpu.HBM)] * 3,
        out_specs=pl.BlockSpec(memory_space=pltpu.VMEM),
        scratch_shapes=[
            pltpu.VMEM(q.shape, jnp.bfloat16),
            pltpu.VMEM((GROUP, kv_heads * head, run), jnp.bfloat16),
            pltpu.VMEM((GROUP, kv_heads * head, run), jnp.bfloat16),
            pltpu.VMEM((GROUP, heads, run), jnp.bfloat16),
            pltpu.VMEM((GROUP, heads, LANES), jnp.float32),
            pltpu.VMEM((GROUP, heads, LANES), jnp.float32),
            pltpu.VMEM((groups, n, GROUP * heads * head // LANES, LANES), jnp.bfloat16),
            pltpu.VMEM((groups, n, 2 * GROUP, LANES), jnp.float32),
            pltpu.SemaphoreType.DMA,
            pltpu.SemaphoreType.DMA((GROUP,)),
            pltpu.SemaphoreType.DMA((GROUP,)),
            pltpu.SemaphoreType.DMA,
            pltpu.SemaphoreType.DMA((groups, n - 1)),
            pltpu.SemaphoreType.DMA,
            pltpu.SemaphoreType.DMA((groups, n - 1)),
        ],
        compiler_params=pltpu.CompilerParams(collective_id=0, has_side_effects=True, vmem_limit_bytes=48 * 2**20),
    )(q, k, v)


def solution(mesh):
    n = mesh.shape["sp"]
    return jax.shard_map(
        functools.partial(attention, n, "sp"),
        mesh=mesh,
        in_specs=(P("dp", None, None), P("dp", "sp", None, None), P("dp", "sp", None, None)),
        out_specs=P("dp", None, None),
        check_vma=False,
    )
```

time: 160 us -> 70.9 us (0.44)
  Pallas kernels: 0 us -> 70 us
  matrix products: 62.1 us -> 0 us
  waiting for transfers between devices: 51.3 us -> 0 us
  other arithmetic: 17.6 us -> 0 us
  local copies, waits for them, and re-layouts: 15.2 us -> 0.8 us
  between operations: 13.5 us -> 0.01 us
    pallas_call x0 -> x1, Pallas kernels: none -> 70 us  [attention(): pl.pallas_call(functools.partial(kernel, n, axis), out_shape=jax.ShapeDty...]
    dot_general x2 -> x0, matrix products: 62.1 us -> none  [einsum(): return jnp.einsum(form, a.astype(jnp.float32), b.astype(jnp.float32))]
    all_gather x1 -> x0, waiting for transfers between devices: 51.3 us -> none  [step(): return together(lax.all_gather(part_of(q, k, v), 'sp')).reshape(q.shape)]
    slice x1 -> x0, other arithmetic: 8.92 us -> none  [together(): seen, total, high = (parts[..., :-2], parts[..., -2:-1], parts[..., -1:])]
    reduce_sum x3 -> x0, other arithmetic: 7.82 us -> none  [the longest x1 4.16 us: together(): jnp.sum(seen * scale, 0) / jnp.sum(total * scale, 0)]
    unnamed x3 -> x1, local copies, waits for them, and re-layouts: 7.41 us -> 0.8 us
    broadcast_in_dim x2 -> x0, local copies, waits for them, and re-layouts: 3.33 us -> none  [the longest x1 1.66 us: part_of(): jnp.sum(weights, -1, keepdims=True)]
  transfers between devices with their start and end apart: 1 -> 0, of which waited for: 1 -> 0; matrix products, arithmetic and copies ran while one was open for 0% -> 0% of each run, Pallas kernels for 0% -> 0%
where the time goes in v1:
time: 70.9 us; the launch traced here: 70.8 us
  Pallas kernels  70 us (99%)
  local copies, waits for them, and re-layouts  0.8 us (1%)
    pallas_call x1, Pallas kernels, attention(): pl.pallas_call(functools.partial(kernel, n, axis), out_shape=jax.ShapeDty...  70 us

profile of v1, /device:TPU:0, one launch (start us, length us, event | category | flops | bytes accessed | tf_op | source)
XLA Modules:
  0.0 70.8 jit_solution(4951331610294739482)
XLA Ops:
  0.0 70.0 %shard_map.37 = bf16[32,32,160]{2,1,0:T(8,128)(2,1)S(1)} custom-call(bf16[32,32,160]{2,1,0:T(8,128)(2,1)} %q_hbm.1, bf16[32,1280,1024]{2,1,0:T(8,128)(2,1)} %bitcast.1.k_hbm, bf16[32,1280,1024]{2,1,0:T(8,128)(2,1)} %bitcast.3.v_hbm), custom_call_target="tpu_custom_call" | custom-call | tf_op jit(solution)/shard_map/pallas_call | solution.py:158
  70.0 0.8 %copy.5 = bf16[32,32,160]{2,1,0:T(8,128)(2,1)} copy(bf16[32,32,160]{2,1,0:T(8,128)(2,1)S(1)} %shard_map.37) | data formatting | bytes 655360

commit v2 on v1

v2 whole, which is shorter than its diff:
```python
import functools

import jax
import jax.numpy as jnp
from jax import lax
from jax.experimental import pallas as pl
from jax.experimental.pallas import tpu as pltpu
from jax.sharding import PartitionSpec as P

GROUP = 4
LANES = 128
MESH = pl.DeviceIdType.MESH


def kernel(n, axis, q_hbm, k_hbm, v_hbm, o_ref, q_buf, k_buf, v_buf, weights, parts, stats, q_sem, k_sem, v_sem,
           part_send, part_recv, late_recv, stat_send, stat_recv):
    seqs, heads, head = q_buf.shape
    wide = k_buf.shape[1]
    kv_heads = wide // head
    share = heads // kv_heads
    fold = LANES // heads
    rows = head // fold
    groups = seqs // GROUP
    me = lax.axis_index(axis)

    barrier = pltpu.get_barrier_semaphore()
    for step in range(1, n):
        pl.semaphore_signal(barrier, inc=1, device_id={axis: lax.rem(me + step, n)}, device_id_type=MESH)

    def k_copy(seq, slot):
        return pltpu.make_async_copy(k_hbm.at[seq], k_buf.at[slot], k_sem.at[slot])

    def v_copy(seq, slot):
        return pltpu.make_async_copy(v_hbm.at[seq], v_buf.at[slot], v_sem.at[slot])

    q_copy = pltpu.make_async_copy(q_hbm, q_buf, q_sem)
    q_copy.start()
    for seq in range(GROUP):
        k_copy(seq, seq).start()
        v_copy(seq, seq).start()
    q_copy.wait()

    row = lax.broadcasted_iota(jnp.int32, (heads, wide), 0)
    lane = lax.broadcasted_iota(jnp.int32, (heads, wide), 1)
    first = (row // share) * head
    own = (lane >= first) & (lane < first + head)
    column = lax.broadcasted_iota(jnp.int32, (heads, LANES), 1)
    of_kv = lax.broadcasted_iota(jnp.int32, (head, heads), 1) // share

    def score(group, slot):
        q = q_buf[group * GROUP + slot].astype(jnp.float32)
        spread = jnp.where(own, jnp.concatenate([q] * kv_heads, axis=1), 0.0).astype(jnp.bfloat16)
        scores = jnp.dot(spread, k_buf[slot], preferred_element_type=jnp.float32) * head**-0.5
        high = jnp.max(scores, axis=1, keepdims=True)
        w = jnp.exp(scores - high)
        weights[slot] = w.astype(jnp.bfloat16)
        turned = jnp.transpose(jnp.where(column == 0, high, jnp.sum(w, axis=1, keepdims=True)))
        stats[group, me, slot] = jnp.concatenate([turned[:2, :]] * fold, axis=1)

    def attend(group, slot):
        w = weights[slot]
        out = None
        for kv in range(kv_heads):
            seen = lax.dot_general(
                v_buf[slot, head * kv : head * (kv + 1), :], w, (((1,), (1,)), ((), ())), preferred_element_type=jnp.float32
            )
            out = seen if out is None else jnp.where(of_kv == kv, seen, out)
        folded = jnp.concatenate([out[rows * f : rows * (f + 1)] for f in range(fold)], axis=1)
        blank = jnp.zeros((parts.shape[3] - rows, LANES), jnp.float32)
        parts[group, me, slot] = jnp.concatenate([folded, blank], axis=0).astype(jnp.bfloat16)

    def spread_out(src, dst, send, recv):
        for step in range(1, n):
            pltpu.make_async_remote_copy(
                src_ref=src,
                dst_ref=dst,
                send_sem=send,
                recv_sem=recv.at[step - 1],
                device_id={axis: lax.rem(me + step, n)},
                device_id_type=MESH,
            ).start()

    def send_part(group, slot, last):
        ref = parts.at[group, me, slot]
        spread_out(ref, ref, part_send, late_recv.at[slot] if last else part_recv.at[group])

    def send_stats(group):
        ref = stats.at[group, me]
        spread_out(ref, ref, stat_send, stat_recv.at[group])

    def arrive(what, recv):
        for step in range(1, n):
            ref = what(lax.rem(me + n - step, n))
            pltpu.make_async_copy(ref, ref, recv.at[step - 1]).wait()

    def combine(group, slot):
        high = [stats[group, d, slot, 0:1, :] for d in range(n)]
        total = [stats[group, d, slot, 1:2, :] for d in range(n)]
        top = functools.reduce(jnp.maximum, high)
        scale = [jnp.exp(h - top) for h in high]
        inverse = 1.0 / functools.reduce(jnp.add, [t * s for t, s in zip(total, scale)])
        out = functools.reduce(
            jnp.add, [parts[group, d, slot, :rows, :].astype(jnp.float32) * (scale[d] * inverse) for d in range(n)]
        )
        turned = jnp.transpose(out)
        o_ref[group * GROUP + slot] = jnp.concatenate(
            [turned[heads * f : heads * (f + 1), :] for f in range(fold)], axis=1
        ).astype(o_ref.dtype)

    def combine_group(group):
        arrive(lambda d: stats.at[group, d], stat_recv.at[group])
        arrive(lambda d: parts.at[group, d], part_recv.at[group])
        for slot in range(GROUP):
            combine(group, slot)

    def run(group, last):
        for slot in range(GROUP):
            seq, ahead = group * GROUP + slot, (slot + 1) % GROUP
            more = not (last and slot == GROUP - 1)
            if more:
                k_copy(seq + 1, ahead).wait()
            v_copy(seq, slot).wait()
            if more:
                score(group + (slot + 1) // GROUP, ahead)
            attend(group, slot)
            if not last:
                @pl.when(seq + 1 + GROUP < seqs)
                def _():
                    k_copy(seq + 1 + GROUP, ahead).start()

                v_copy(seq + GROUP, slot).start()
            if isinstance(group, int) and group == 0 and slot == 0:
                pl.semaphore_wait(barrier, n - 1)
            send_part(group, slot, last)
            if slot == GROUP - 2:
                send_stats(group)

    k_copy(0, 0).wait()
    score(0, 0)
    k_copy(GROUP, 0).start()
    run(0, False)

    def middle(group, carry):
        run(group, False)
        combine_group(group - 1)
        return carry

    lax.fori_loop(1, groups - 1, middle, 0)
    run(groups - 1, True)
    combine_group(groups - 2)
    arrive(lambda d: stats.at[groups - 1, d], stat_recv.at[groups - 1])
    for slot in range(GROUP):
        arrive(lambda d: parts.at[groups - 1, d, slot], late_recv.at[slot])
        combine(groups - 1, slot)
    for what, send in ((parts, part_send), (stats, stat_send)):
        ref = what.at[:, pl.ds(0, n - 1)]
        pltpu.make_async_copy(ref, ref, send).wait()


def attention(n, axis, q, k, v):
    seqs, run, kv_heads, head = k.shape
    heads = q.shape[1]
    groups = seqs // GROUP
    rows = -(-heads * head // LANES // 16) * 16
    k, v = (x.transpose(0, 2, 3, 1).reshape(seqs, kv_heads * head, run) for x in (k, v))
    q, k, v = (pltpu.with_memory_space_constraint(x, pltpu.HBM) for x in (q, k, v))
    return pl.pallas_call(
        functools.partial(kernel, n, axis),
        out_shape=jax.ShapeDtypeStruct(q.shape, jnp.bfloat16),
        in_specs=[pl.BlockSpec(memory_space=pltpu.HBM)] * 3,
        out_specs=pl.BlockSpec(memory_space=pltpu.VMEM),
        scratch_shapes=[
            pltpu.VMEM(q.shape, jnp.bfloat16),
            pltpu.VMEM((GROUP, kv_heads * head, run), jnp.bfloat16),
            pltpu.VMEM((GROUP, kv_heads * head, run), jnp.bfloat16),
            pltpu.VMEM((GROUP, heads, run), jnp.bfloat16),
            pltpu.VMEM((groups, n, GROUP, rows, LANES), jnp.bfloat16),
            pltpu.VMEM((groups, n, GROUP, 2, LANES), jnp.float32),
            pltpu.SemaphoreType.DMA,
            pltpu.SemaphoreType.DMA((GROUP,)),
            pltpu.SemaphoreType.DMA((GROUP,)),
            pltpu.SemaphoreType.DMA,
            pltpu.SemaphoreType.DMA((groups, n - 1)),
            pltpu.SemaphoreType.DMA((GROUP, n - 1)),
            pltpu.SemaphoreType.DMA,
            pltpu.SemaphoreType.DMA((groups, n - 1)),
        ],
        compiler_params=pltpu.CompilerParams(collective_id=0, has_side_effects=True, vmem_limit_bytes=48 * 2**20),
    )(q, k, v)


def solution(mesh):
    n = mesh.shape["sp"]
    return jax.shard_map(
        functools.partial(attention, n, "sp"),
        mesh=mesh,
        in_specs=(P("dp", None, None), P("dp", "sp", None, None), P("dp", "sp", None, None)),
        out_specs=P("dp", None, None),
        check_vma=False,
    )
```

time: 70.9 us -> 62.5 us (0.88)
  Pallas kernels: 70 us -> 61.6 us
    pallas_call x1, Pallas kernels: 70 us -> 61.6 us  [attention(): pl.pallas_call(functools.partial(kernel, n, axis), out_shape=jax.ShapeDty...]
where the time goes in v2:
time: 62.5 us; the launch traced here: 62.4 us
  Pallas kernels  61.6 us (99%)
  local copies, waits for them, and re-layouts  0.8 us (1%)
    pallas_call x1, Pallas kernels, attention(): pl.pallas_call(functools.partial(kernel, n, axis), out_shape=jax.ShapeDty...  61.6 us

profile of v2, /device:TPU:0, one launch (start us, length us, event | category | flops | bytes accessed | tf_op | source)
XLA Modules:
  0.0 62.4 jit_solution(1354316971110888823)
XLA Ops:
  0.0 61.6 %shard_map.37 = bf16[32,32,160]{2,1,0:T(8,128)(2,1)S(1)} custom-call(bf16[32,32,160]{2,1,0:T(8,128)(2,1)} %q_hbm.1, bf16[32,1280,1024]{2,1,0:T(8,128)(2,1)} %bitcast.1.k_hbm, bf16[32,1280,1024]{2,1,0:T(8,128)(2,1)} %bitcast.3.v_hbm), custom_call_target="tpu_custom_call" | custom-call | tf_op jit(solution)/shard_map/pallas_call | solution.py:167
  61.6 0.8 %copy.5 = bf16[32,32,160]{2,1,0:T(8,128)(2,1)} copy(bf16[32,32,160]{2,1,0:T(8,128)(2,1)S(1)} %shard_map.37) | data formatting | bytes 655360

commit v3 on v2

--- a/solution.py
+++ b/solution.py
@@ -80,9 +80,9 @@
                 device_id_type=MESH,
             ).start()
 
-    def send_part(group, slot, last):
-        ref = parts.at[group, me, slot]
-        spread_out(ref, ref, part_send, late_recv.at[slot] if last else part_recv.at[group])
+    def send_parts(group, first, count, recv):
+        ref = parts.at[group, me, pl.ds(first, count)]
+        spread_out(ref, ref, part_send, recv)
 
     def send_stats(group):
         ref = stats.at[group, me]
@@ -107,19 +107,21 @@
             [turned[heads * f : heads * (f + 1), :] for f in range(fold)], axis=1
         ).astype(o_ref.dtype)
 
-    def combine_group(group):
+    def arrive_group(group):
         arrive(lambda d: stats.at[group, d], stat_recv.at[group])
         arrive(lambda d: parts.at[group, d], part_recv.at[group])
-        for slot in range(GROUP):
-            combine(group, slot)
-
-    def run(group, last):
+
+    def run(group, mix, last=False, start=False):
         for slot in range(GROUP):
             seq, ahead = group * GROUP + slot, (slot + 1) % GROUP
             more = not (last and slot == GROUP - 1)
+            if mix and slot == 0:
+                arrive_group(group - 2)
             if more:
                 k_copy(seq + 1, ahead).wait()
             v_copy(seq, slot).wait()
+            if mix:
+                combine(group - 2, slot)
             if more:
                 score(group + (slot + 1) // GROUP, ahead)
             attend(group, slot)
@@ -129,25 +131,25 @@
                     k_copy(seq + 1 + GROUP, ahead).start()
 
                 v_copy(seq + GROUP, slot).start()
-            if isinstance(group, int) and group == 0 and slot == 0:
+            if start and slot == 0:
                 pl.semaphore_wait(barrier, n - 1)
-            send_part(group, slot, last)
+            if last:
+                send_parts(group, slot, 1, late_recv.at[slot])
+            elif slot % 2:
+                send_parts(group, slot - 1, 2, part_recv.at[group])
             if slot == GROUP - 2:
                 send_stats(group)
 
     k_copy(0, 0).wait()
     score(0, 0)
     k_copy(GROUP, 0).start()
-    run(0, False)
-
-    def middle(group, carry):
-        run(group, False)
-        combine_group(group - 1)
-        return carry
-
-    lax.fori_loop(1, groups - 1, middle, 0)
-    run(groups - 1, True)
-    combine_group(groups - 2)
+    run(0, False, start=True)
+    run(1, False)
+    lax.fori_loop(2, groups - 1, lambda group, carry: (run(group, True), carry)[1], 0)
+    run(groups - 1, True, last=True)
+    arrive_group(groups - 2)
+    for slot in range(GROUP):
+        combine(groups - 2, slot)
     arrive(lambda d: stats.at[groups - 1, d], stat_recv.at[groups - 1])
     for slot in range(GROUP):
         arrive(lambda d: parts.at[groups - 1, d, slot], late_recv.at[slot])

time: 62.5 us -> 60.2 us (0.963)
  Pallas kernels: 61.6 us -> 59.3 us
    pallas_call x1, Pallas kernels: 61.6 us -> 59.3 us  [attention(): pl.pallas_call(functools.partial(kernel, n, axis), out_shape=jax.ShapeDty...]
where the time goes in v3:
time: 60.2 us; the launch traced here: 60.1 us
  Pallas kernels  59.3 us (99%)
  local copies, waits for them, and re-layouts  0.8 us (1%)
    pallas_call x1, Pallas kernels, attention(): pl.pallas_call(functools.partial(kernel, n, axis), out_shape=jax.ShapeDty...  59.3 us

profile of v3, /device:TPU:0, one launch (start us, length us, event | category | flops | bytes accessed | tf_op | source)
XLA Modules:
  0.0 60.1 jit_solution(3555104018196477232)
XLA Ops:
  0.0 59.3 %shard_map.37 = bf16[32,32,160]{2,1,0:T(8,128)(2,1)S(1)} custom-call(bf16[32,32,160]{2,1,0:T(8,128)(2,1)} %q_hbm.1, bf16[32,1280,1024]{2,1,0:T(8,128)(2,1)} %bitcast.1.k_hbm, bf16[32,1280,1024]{2,1,0:T(8,128)(2,1)} %bitcast.3.v_hbm), custom_call_target="tpu_custom_call" | custom-call | tf_op jit(solution)/shard_map/pallas_call | solution.py:169
  59.3 0.8 %copy.5 = bf16[32,32,160]{2,1,0:T(8,128)(2,1)} copy(bf16[32,32,160]{2,1,0:T(8,128)(2,1)S(1)} %shard_map.37) | data formatting | bytes 655360

commit v4 on v3

--- a/solution.py
+++ b/solution.py
@@ -23,21 +23,23 @@
     groups = seqs // GROUP
     me = lax.axis_index(axis)
 
+    def k_copy(seq, slot):
+        return pltpu.make_async_copy(k_hbm.at[seq], k_buf.at[slot], k_sem.at[slot])
+
+    def v_copy(seq, slot):
+        return pltpu.make_async_copy(v_hbm.at[seq], v_buf.at[slot], v_sem.at[slot])
+
+    q_copy = pltpu.make_async_copy(q_hbm, q_buf, q_sem)
+    k_copy(0, 0).start()
+    q_copy.start()
+    v_copy(0, 0).start()
+    for seq in range(1, GROUP):
+        k_copy(seq, seq).start()
+        v_copy(seq, seq).start()
+
     barrier = pltpu.get_barrier_semaphore()
     for step in range(1, n):
         pl.semaphore_signal(barrier, inc=1, device_id={axis: lax.rem(me + step, n)}, device_id_type=MESH)
-
-    def k_copy(seq, slot):
-        return pltpu.make_async_copy(k_hbm.at[seq], k_buf.at[slot], k_sem.at[slot])
-
-    def v_copy(seq, slot):
-        return pltpu.make_async_copy(v_hbm.at[seq], v_buf.at[slot], v_sem.at[slot])
-
-    q_copy = pltpu.make_async_copy(q_hbm, q_buf, q_sem)
-    q_copy.start()
-    for seq in range(GROUP):
-        k_copy(seq, seq).start()
-        v_copy(seq, seq).start()
     q_copy.wait()
 
     row = lax.broadcasted_iota(jnp.int32, (heads, wide), 0)
@@ -69,14 +71,16 @@
         blank = jnp.zeros((parts.shape[3] - rows, LANES), jnp.float32)
         parts[group, me, slot] = jnp.concatenate([folded, blank], axis=0).astype(jnp.bfloat16)
 
+    peers = sorted(range(1, n), key=lambda bits: (-(bits // 2).bit_count(), bits % 2))
+
     def spread_out(src, dst, send, recv):
-        for step in range(1, n):
+        for at, bits in enumerate(peers):
             pltpu.make_async_remote_copy(
                 src_ref=src,
                 dst_ref=dst,
                 send_sem=send,
-                recv_sem=recv.at[step - 1],
-                device_id={axis: lax.rem(me + step, n)},
+                recv_sem=recv.at[at],
+                device_id={axis: me ^ bits},
                 device_id_type=MESH,
             ).start()
 
@@ -89,19 +93,21 @@
         spread_out(ref, ref, stat_send, stat_recv.at[group])
 
     def arrive(what, recv):
-        for step in range(1, n):
-            ref = what(lax.rem(me + n - step, n))
-            pltpu.make_async_copy(ref, ref, recv.at[step - 1]).wait()
-
-    def combine(group, slot):
+        for at, bits in reversed(list(enumerate(peers))):
+            ref = what(me ^ bits)
+            pltpu.make_async_copy(ref, ref, recv.at[at]).wait()
+
+    def factors(group, slot):
         high = [stats[group, d, slot, 0:1, :] for d in range(n)]
         total = [stats[group, d, slot, 1:2, :] for d in range(n)]
         top = functools.reduce(jnp.maximum, high)
         scale = [jnp.exp(h - top) for h in high]
         inverse = 1.0 / functools.reduce(jnp.add, [t * s for t, s in zip(total, scale)])
-        out = functools.reduce(
-            jnp.add, [parts[group, d, slot, :rows, :].astype(jnp.float32) * (scale[d] * inverse) for d in range(n)]
-        )
+        return [s * inverse for s in scale]
+
+    def combine(group, slot, shares=None):
+        shares = shares or factors(group, slot)
+        out = functools.reduce(jnp.add, [parts[group, d, slot, :rows, :].astype(jnp.float32) * shares[d] for d in range(n)])
         turned = jnp.transpose(out)
         o_ref[group * GROUP + slot] = jnp.concatenate(
             [turned[heads * f : heads * (f + 1), :] for f in range(fold)], axis=1
@@ -151,9 +157,10 @@
     for slot in range(GROUP):
         combine(groups - 2, slot)
     arrive(lambda d: stats.at[groups - 1, d], stat_recv.at[groups - 1])
+    shares = [factors(groups - 1, slot) for slot in range(GROUP)]
     for slot in range(GROUP):
         arrive(lambda d: parts.at[groups - 1, d, slot], late_recv.at[slot])
-        combine(groups - 1, slot)
+        combine(groups - 1, slot, shares[slot])
     for what, send in ((parts, part_send), (stats, stat_send)):
         ref = what.at[:, pl.ds(0, n - 1)]
         pltpu.make_async_copy(ref, ref, send).wait()

time: 60.2 us -> 60.2 us (level)
  no operation moved by 1% of the time
where the time goes in v4:
time: 60.2 us; the launch traced here: 60.1 us
  Pallas kernels  59.3 us (99%)
  local copies, waits for them, and re-layouts  0.8 us (1%)
    pallas_call x1, Pallas kernels, attention(): pl.pallas_call(functools.partial(kernel, n, axis), out_shape=jax.ShapeDty...  59.3 us

profile of v4, /device:TPU:0, one launch (start us, length us, event | category | flops | bytes accessed | tf_op | source)
XLA Modules:
  0.0 60.1 jit_solution(15498649618971055817)
XLA Ops:
  0.0 59.3 %shard_map.37 = bf16[32,32,160]{2,1,0:T(8,128)(2,1)S(1)} custom-call(bf16[32,32,160]{2,1,0:T(8,128)(2,1)} %q_hbm.1, bf16[32,1280,1024]{2,1,0:T(8,128)(2,1)} %bitcast.1.k_hbm, bf16[32,1280,1024]{2,1,0:T(8,128)(2,1)} %bitcast.3.v_hbm), custom_call_target="tpu_custom_call" | custom-call | tf_op jit(solution)/shard_map/pallas_call | solution.py:176
  59.3 0.8 %copy.5 = bf16[32,32,160]{2,1,0:T(8,128)(2,1)} copy(bf16[32,32,160]{2,1,0:T(8,128)(2,1)S(1)} %shard_map.37) | data formatting | bytes 655360

commit v5 on v4

--- a/solution.py
+++ b/solution.py
@@ -47,7 +47,6 @@
     first = (row // share) * head
     own = (lane >= first) & (lane < first + head)
     column = lax.broadcasted_iota(jnp.int32, (heads, LANES), 1)
-    of_kv = lax.broadcasted_iota(jnp.int32, (head, heads), 1) // share
 
     def score(group, slot):
         q = q_buf[group * GROUP + slot].astype(jnp.float32)
@@ -59,15 +58,21 @@
         turned = jnp.transpose(jnp.where(column == 0, high, jnp.sum(w, axis=1, keepdims=True)))
         stats[group, me, slot] = jnp.concatenate([turned[:2, :]] * fold, axis=1)
 
-    def attend(group, slot):
-        w = weights[slot]
+    def attend(group, slot, repeat=False):
+        w = jnp.concatenate([weights[slot]] * (fold if repeat else 1), axis=0)
+        of_kv = lax.broadcasted_iota(jnp.int32, (head, w.shape[0]), 1) % heads // share
         out = None
         for kv in range(kv_heads):
             seen = lax.dot_general(
                 v_buf[slot, head * kv : head * (kv + 1), :], w, (((1,), (1,)), ((), ())), preferred_element_type=jnp.float32
             )
             out = seen if out is None else jnp.where(of_kv == kv, seen, out)
-        folded = jnp.concatenate([out[rows * f : rows * (f + 1)] for f in range(fold)], axis=1)
+        pieces = [out[rows * f : rows * (f + 1)] for f in range(fold)]
+        if repeat:
+            at = lax.broadcasted_iota(jnp.int32, (rows, LANES), 1) // heads
+            folded = functools.reduce(lambda got, f: jnp.where(at == f, pieces[f], got), range(1, fold), pieces[0])
+        else:
+            folded = jnp.concatenate(pieces, axis=1)
         blank = jnp.zeros((parts.shape[3] - rows, LANES), jnp.float32)
         parts[group, me, slot] = jnp.concatenate([folded, blank], axis=0).astype(jnp.bfloat16)
 
@@ -130,7 +135,7 @@
                 combine(group - 2, slot)
             if more:
                 score(group + (slot + 1) // GROUP, ahead)
-            attend(group, slot)
+            attend(group, slot, not more)
             if not last:
                 @pl.when(seq + 1 + GROUP < seqs)
                 def _():
@@ -152,10 +157,11 @@
     run(0, False, start=True)
     run(1, False)
     lax.fori_loop(2, groups - 1, lambda group, carry: (run(group, True), carry)[1], 0)
-    run(groups - 1, True, last=True)
-    arrive_group(groups - 2)
-    for slot in range(GROUP):
-        combine(groups - 2, slot)
+    run(groups - 1, False, last=True)
+    for group in (groups - 3, groups - 2):
+        arrive_group(group)
+        for slot in range(GROUP):
+            combine(group, slot)
     arrive(lambda d: stats.at[groups - 1, d], stat_recv.at[groups - 1])
     shares = [factors(groups - 1, slot) for slot in range(GROUP)]
     for slot in range(GROUP):

time: 60.2 us -> 60.2 us (level)
  no operation moved by 1% of the time
where the time goes in v5:
time: 60.2 us; the launch traced here: 60.1 us
  Pallas kernels  59.3 us (99%)
  local copies, waits for them, and re-layouts  0.8 us (1%)
    pallas_call x1, Pallas kernels, attention(): pl.pallas_call(functools.partial(kernel, n, axis), out_shape=jax.ShapeDty...  59.3 us

profile of v5, /device:TPU:0, one launch (start us, length us, event | category | flops | bytes accessed | tf_op | source)
XLA Modules:
  0.0 60.1 jit_solution(8898567311589162315)
XLA Ops:
  0.0 59.3 %shard_map.37 = bf16[32,32,160]{2,1,0:T(8,128)(2,1)S(1)} custom-call(bf16[32,32,160]{2,1,0:T(8,128)(2,1)} %q_hbm.1, bf16[32,1280,1024]{2,1,0:T(8,128)(2,1)} %bitcast.1.k_hbm, bf16[32,1280,1024]{2,1,0:T(8,128)(2,1)} %bitcast.3.v_hbm), custom_call_target="tpu_custom_call" | custom-call | tf_op jit(solution)/shard_map/pallas_call | solution.py:182
  59.3 0.8 %copy.5 = bf16[32,32,160]{2,1,0:T(8,128)(2,1)} copy(bf16[32,32,160]{2,1,0:T(8,128)(2,1)S(1)} %shard_map.37) | data formatting | bytes 655360
